TPU v7x, 32 devices: a whole 2x2x4 slice. The times are simulated.
32 devices in a mesh: seq: 16 (over z, x, core), head: 1, batch: 2 (over y).
Axes of the slice: x: 2, y: 2, z: 4, core: 2. Of those that a mesh axis runs over, the one named last changes fastest.
Arguments:
- queries: bfloat16 [2, 8192, 8, 8, 128], P('batch', 'seq', 'head'), may hold values from -160 to 160
- key_rows: bfloat16 [2, 8192, 8, 128], P('batch', 'seq'), may hold values from -6 to 6
- value_rows: bfloat16 [2, 8192, 8, 128], P('batch', 'seq'), may hold values from -6 to 6
- compressed: bfloat16 [2, 128, 8, 128], P('batch', 'seq'), may hold values from -6 to 6
- chosen: int32 [2, 128, 8, 16], P('batch', 'seq'), may hold values from 0 to 127, as said below
Outputs:
- block_scores: float32 [2, 128, 8, 128], P('batch', 'seq', 'head')
- attended: bfloat16 [2, 8192, 8, 8, 128], P('batch', 'seq', 'head')
Inputs may be any that keep to these rules, and one draw needn't show every extreme that they name: `chosen`: every entry is at most its own tile number, and entry 0 of every row is the tile's own block. Over the tiles of one device of seq and one group, at most 2 different blocks of any other device are named, and every device after the first names exactly 2 blocks of the first device for each group.
All inputs are finite; a program needn't handle non-finite values.
Results may differ from a plain program's by a relative error of at most 0.008.
Values may be sent and summed in bfloat16 or wider, within the bound.
A program may use at most 128 MiB of HBM per device.

v0:
```python
import jax
import jax.numpy as jnp
from jax import lax
from jax.sharding import PartitionSpec as P

HPG = 8
BLOCK = 64
TOPN = 16
CAP = 2


def softmax_parts(scores):
    row_top = jnp.max(scores, axis=-1, keepdims=True)
    weights = jnp.exp(scores - row_top)
    return (weights, jnp.sum(weights, axis=-1, keepdims=True))


def local(queries, key_rows, value_rows, compressed, chosen):
    _, tok_rows, heads_local, groups, head_width = queries.shape
    block_len = BLOCK
    shards = lax.axis_size("seq")
    seq_rank = lax.axis_index("seq")
    blk_dev = tok_rows // block_len
    nblk = blk_dev * shards
    score_scale = head_width ** (-0.5)
    query_rows = queries[0]
    query_pos = seq_rank * tok_rows + jnp.arange(tok_rows, dtype=jnp.int32)
    logits = (
        jnp.einsum(
            "tjgd,ngd->tjgn",
            query_rows,
            lax.all_gather(compressed, "seq", axis=1, tiled=True)[0],
            preferred_element_type=jnp.float32,
        )
        * score_scale
    )
    all_blocks = jnp.arange(nblk, dtype=jnp.int32)
    seen = all_blocks[None, :] <= (query_pos // block_len)[:, None]
    logits = jnp.where(seen[:, None, None, :], logits, -jnp.inf)
    weights, totals = softmax_parts(logits)
    probability = weights / totals
    pooled = jnp.sum(
        probability.reshape(blk_dev, block_len, heads_local, groups, nblk), axis=(1, 2)
    )[None]
    shared = lax.psum_scatter(
        pooled.astype(jnp.bfloat16), "head", scatter_dimension=2, tiled=True
    ).astype(jnp.float32)
    tile_ids = seq_rank * blk_dev + jnp.arange(blk_dev, dtype=jnp.int32)
    factor = (tile_ids + 1).astype(jnp.float32) / (block_len * HPG)
    block_scores = shared * factor[None, :, None, None]
    pick_rows = chosen[0]
    onehot = pick_rows[..., None] == all_blocks
    needed = jnp.any(onehot, axis=(0, 2))
    owner_of = all_blocks // blk_dev
    needed = needed & (owner_of != seq_rank)[None, :]
    needed_grid = needed.reshape(groups, shards, blk_dev).astype(jnp.int32)
    rank_in = jnp.cumsum(needed_grid, axis=2) - needed_grid
    places = jnp.arange(CAP, dtype=jnp.int32)
    within = jnp.arange(blk_dev, dtype=jnp.int32)
    matched = (needed_grid[..., None] == 1) & (rank_in[..., None] == places)
    wanted = jnp.sum(jnp.where(matched, within[:, None], 0), axis=2)
    slot_of = blk_dev + owner_of[None, :] * CAP + rank_in.reshape(groups, nblk)
    slot_of = jnp.where(
        owner_of[None, :] == seq_rank, all_blocks[None, :] - seq_rank * blk_dev, slot_of
    )
    pool_index = jnp.sum(jnp.where(onehot, slot_of[None, :, None, :], 0), axis=3)
    key_local = key_rows[0].reshape(blk_dev, block_len, groups, head_width)
    value_local = value_rows[0].reshape(blk_dev, block_len, groups, head_width)
    requested = lax.all_to_all(wanted, "seq", split_axis=1, concat_axis=1, tiled=True)
    group_ids = jnp.arange(requested.shape[0], dtype=jnp.int32)[:, None, None]
    found = jnp.concatenate(
        [key_local[requested, :, group_ids, :], value_local[requested, :, group_ids, :]], axis=-1
    )
    fetched = lax.all_to_all(found, "seq", split_axis=1, concat_axis=1, tiled=True)
    key_remote = fetched[..., :head_width].reshape(groups, shards * CAP, block_len, head_width)
    value_remote = fetched[..., head_width:].reshape(groups, shards * CAP, block_len, head_width)
    key_pool = jnp.concatenate([jnp.transpose(key_local, (2, 0, 1, 3)), key_remote], axis=1)
    value_pool = jnp.concatenate([jnp.transpose(value_local, (2, 0, 1, 3)), value_remote], axis=1)
    tile_step = 2
    rounds = blk_dev // tile_step
    group_sel = jnp.arange(groups, dtype=jnp.int32)[None, :, None]

    def attend(inputs):
        query_part, index_part, pick_part, pos_part = inputs
        key_sel = key_pool[group_sel, index_part].reshape(
            tile_step, groups, TOPN * block_len, head_width
        )
        value_sel = value_pool[group_sel, index_part].reshape(
            tile_step, groups, TOPN * block_len, head_width
        )
        key_pos = (
            pick_part[..., None] * block_len + jnp.arange(block_len, dtype=jnp.int32)
        ).reshape(tile_step, groups, TOPN * block_len)
        scores = (
            jnp.einsum("tqhgd,tgkd->tghqk", query_part, key_sel, preferred_element_type=jnp.float32)
            * score_scale
        )
        visible = key_pos[:, :, None, None, :] <= pos_part[:, None, None, :, None]
        scores = jnp.where(visible, scores, -jnp.inf)
        weights, totals = softmax_parts(scores)
        rounded = weights.astype(jnp.bfloat16)
        mixed = jnp.einsum(
            "tghqk,tgkd->tqhgd", rounded, value_sel, preferred_element_type=jnp.float32
        )
        return (mixed / jnp.transpose(totals, (0, 3, 2, 1, 4))).astype(jnp.bfloat16)

    attended = lax.map(
        attend,
        (
            query_rows.reshape(rounds, tile_step, block_len, heads_local, groups, head_width),
            pool_index.reshape(rounds, tile_step, groups, TOPN),
            pick_rows.reshape(rounds, tile_step, groups, TOPN),
            query_pos.reshape(rounds, tile_step, block_len),
        ),
    )
    attended = attended.reshape(1, tok_rows, heads_local, groups, head_width)
    return (block_scores, attended)


def solution(mesh):
    placed = (
        P("batch", "seq", "head", None, None),
        P("batch", "seq", None, None),
        P("batch", "seq", None, None),
        P("batch", "seq", None, None),
        P("batch", "seq", None, None),
    )
    return jax.shard_map(
        local,
        mesh=mesh,
        in_specs=placed,
        out_specs=(P("batch", "seq", "head", None), P("batch", "seq", "head", None, None)),
        check_vma=False,
    )
```

profile of v0, /device:TPU:15, one launch (start us, length us, event | category | flops | bytes accessed | tf_op | source)
XLA Modules:
  0.0 596.4 jit_solution(10941132345338593036)
XLA Ops:
  0.7 1.0 fusion.30
  1.6 0.1 reduce_or.12
  1.8 1.3 reduce_window_sum.13
  3.3 0.7 copy.57
  4.0 6.5 %all-to-all-start = ((s32[8,16,2]{0,2,1:T(2,128)}), s32[8,16,2]{0,2,1:T(2,128)S(1)}, u32[]{:S(2)}, u32[]{:S(2)}) async-start(s32[8,16,2]{0,2,1:T(2,128)} %copy.57), calls=%async_computation | async-start | bytes 32768 | tf_op jit(solution)/shard_map/all_to_all | solution.py:69
  10.5 1.4 copy.54
  11.9 1.4 copy.53
  13.3 1.4 all-to-all-done
  14.8 0.1 copy.61
  14.9 0.1 reshape.308
  15.0 3.4 gather_fusion.2
  18.4 3.3 gather_fusion.3
  21.7 9.0 %pad_maximum_fusion = bf16[8,16,2,64,256]{4,3,2,1,0:T(8,128)(2,1)} fusion(bf16[8,16,2,64,128]{4,3,2,1,0:T(8,128)(2,1)} %bitcast.144, bf16[8,16,2,64,128]{4,3,2,1,0:T(8,128)(2,1)} %bitcast.143), kind=kLoop, calls=%fused_computation.38 | loop fusion | flops 16777216 | bytes 16777216 | tf_op jit(solution)/shard_map/concatenate | solution.py:71
  30.7 8.2 %copy.62 = bf16[8,16,2,64,256]{4,3,2,0,1:T(8,128)(2,1)} copy(bf16[8,16,2,64,256]{4,3,2,1,0:T(8,128)(2,1)} %pad_maximum_fusion) | data formatting | bytes 16777216 | tf_op jit(solution)/shard_map/concatenate | solution.py:71
  38.9 7.1 %all-to-all-start.1 = ((bf16[8,16,2,64,256]{4,3,2,0,1:T(8,128)(2,1)}), bf16[8,16,2,64,256]{4,3,2,0,1:T(8,128)(2,1)}, u32[]{:S(2)}, u32[]{:S(2)}) async-start(bf16[8,16,2,64,256]{4,3,2,0,1:T(8,128)(2,1)} %copy.62), calls=%async_computation.1 | async-start | bytes 16777216 | tf_op jit(solution)/shard_map/all_to_all | solution.py:74
  46.1 192.4 %all_gather.3 = bf16[1,128,8,128]{3,1,2,0:T(8,128)(2,1)S(1)} all-gather(bf16[1,8,8,128]{3,1,2,0:T(8,128)(2,1)S(1)} %copy.50), channel_id=1, replica_groups=mesh['seq'=16,'head'=1,'batch'=2] {'seq'}, dimensions={1}, use_global_device_ids=true | all-gather | bytes 278528 | tf_op jit(solution)/shard_map/all_gather | solution.py:32
  238.5 39.5 %fusion.25 = f32[8,128,512,8]{2,1,3,0:T(8,128)} fusion(bf16[512,8,8,128]{3,2,1,0:T(8,128)(2,1)} %bitcast.135, bf16[1,128,8,128]{3,1,2,0:T(8,128)(2,1)S(1)} %all_gather.3), kind=kOutput, calls=%fused_computation.39 | convolution fusion | flops 1073741824 | bytes 25427968 | tf_op jit(solution)/shard_map/tjgd,ngd->tjgn/dot_general | solution.py:29
  278.1 17.2 %fusion.22 = f32[512,8,8,128]{0,3,1,2:T(8,128)} fusion(f32[8,128,512,8]{2,1,3,0:T(8,128)} %fusion.25, pred[512,128]{0,1:T(8,128)(4,1)S(1)} %iota_compare_fusion.1), kind=kOutput, calls=%fused_computation.32 | output fusion | flops 21037312 | bytes 33619968 | tf_op jit(solution)/shard_map/div | solution.py:41
  295.3 20.3 %divide_reduce_fusion = f32[512,8,128]{0,2,1:T(8,128)} fusion(f32[512,8,8,128]{0,3,1,2:T(8,128)} %fusion.22, f32[8,128,512,8]{2,1,3,0:T(8,128)} %fusion.25, pred[512,128]{0,1:T(8,128)(4,1)S(1)} %iota_compare_fusion.1), kind=kOutput, calls=%fused_computation.36 | output fusion | flops 28868736 | bytes 35717120 | tf_op jit(solution)/shard_map/sub | solution.py:14
  315.6 3.0 copy.52
  318.7 1.3 select_reduce_fusion
  320.0 1.7 bitcast_reduce_fusion
  321.7 0.7 convert_multiply_fusion
  322.4 4.4 fusion.50
  326.8 1.8 copy.73
  328.7 1.8 copy.74
  330.5 5.5 pad_maximum_fusion.1
  336.0 260.0 %while.11 = (s32[]{:T(128)}, bf16[4,2,64,8,8,128]{5,4,3,2,1,0:T(8,128)(2,1)}, s32[4,2,8,16]{3,2,1,0:T(8,128)S(1)}, bf16[8,40,64,128]{3,2,1,0:T(8,128)(2,1)}, s32...) while((s32[]{:T(128)}, ...), condition=%wide.region_11.12_spmd.clone, body=%wide.region_8.11_spmd.clone.sunk | while | flops 4390389760 | bytes 143193264 | solution.py:107
  336.3 0.1 add.210
  336.5 0.6 broadcast_compare_fusion.4
  337.3 6.0 %gather_fusion = bf16[256,64,128]{2,1,0:T(8,128)(2,1)} fusion(bf16[8,40,64,128]{3,2,1,0:T(8,128)(2,1)} %get-tuple-element.213, s32[256]{0:T(256)S(1)} %reshape.347), kind=kCustom, calls=%fused_computation.1.clone.clone.1 | custom fusion | bytes 8390656 | tf_op jit(solution)/shard_map/while/body/eval_jaxpr/gather | solution.py:85
  343.3 1.8 constant_dynamic-slice_fusion.3
  345.0 16.8 %fusion.68 = (f32[2,8,8,64]{3,2,1,0:T(8,128)S(1)}, f32[2,8,1024,64,8]{2,3,4,1,0:T(8,128)}) fusion(pred[2,8,64,1024]{3,2,1,0:T(8,128)(4,1)S(1)} %broadcast_compare_fusion.4, bf16[2,8,1024,128,1]{3,2,4,1,0:T(8,128)(2,1)} %bitcast.133, bf16[1,2,64,8,8,128]{5,4,3,2,1,0:T(8,128)(2,1)S(1)} %constant_dynamic-slice_fusion.3), kind=kOutput, calls=%fused_computation.9.clone.1 | convolution fusion | flops 2172641280 | bytes 40927232 | tf_op jit(solution)/shard_map/while/body/eval_jaxpr/tqhgd,tgkd->tghqk/dot_general | solution.py:95
  361.8 14.9 %fusion.69 = f32[2,8,8,64]{3,2,1,0:T(8,128)S(1)} fusion(f32[2,8,1024,64,8]{2,3,4,1,0:T(8,128)} %get-tuple-element.187, f32[2,8,8,64]{3,2,1,0:T(8,128)S(1)} %get-tuple-element.188, pred[2,8,64,1024]{3,2,1,0:T(8,128)(4,1)S(1)} %broadcast_compare_fusion.4), kind=kLoop, calls=%fused_computation.7.clone.1 | loop fusion | flops 33546240 | bytes 34668544 | tf_op jit(solution)/shard_map/while/body/eval_jaxpr/reduce_sum | solution.py:15
  376.7 6.0 %gather_fusion.1 = bf16[256,64,128]{2,1,0:T(8,128)(2,1)} fusion(bf16[8,40,64,128]{3,2,1,0:T(8,128)(2,1)} %get-tuple-element.210, s32[256]{0:T(256)S(1)} %reshape.347), kind=kCustom, calls=%fused_computation.clone.clone.1 | custom fusion | bytes 8390656 | tf_op jit(solution)/shard_map/while/body/eval_jaxpr/gather | solution.py:88
  382.7 15.8 %fusion.70 = bf16[1,2,64,8,8,128]{5,2,3,4,1,0:T(8,128)(2,1)S(1)} fusion(f32[2,64,8,8]{1,2,3,0:T(8,128)S(1)} %bitcast.145, bf16[2,8,1024,128,1]{3,2,4,1,0:T(8,128)(2,1)} %bitcast.134, f32[2,8,1024,64,8]{2,3,4,1,0:T(8,128)} %get-tuple-element.187, f32[2,8,8,64]{3,2,1,0:T(8,128)S(1)} %get-tuple-element.188, ...), kind=kOutput, calls=%fused_computation.18.clone.1 | convolution fusion | flops 2183135232 | bytes 40960000 | tf_op jit(solution)/shard_map/while/body/eval_jaxpr/tghqk,tgkd->tqhgd/dot_general | solution.py:102
  398.5 2.7 copy_dynamic-update-slice_fusion.2
  401.2 0.1 add.210
  401.4 0.6 broadcast_compare_fusion.4
  402.2 6.0 %gather_fusion = bf16[256,64,128]{2,1,0:T(8,128)(2,1)} fusion(bf16[8,40,64,128]{3,2,1,0:T(8,128)(2,1)} %get-tuple-element.213, s32[256]{0:T(256)S(1)} %reshape.347), kind=kCustom, calls=%fused_computation.1.clone.clone.1 | custom fusion | bytes 8390656 | tf_op jit(solution)/shard_map/while/body/eval_jaxpr/gather | solution.py:85
  408.2 1.8 constant_dynamic-slice_fusion.3
  410.0 16.8 %fusion.68 = (f32[2,8,8,64]{3,2,1,0:T(8,128)S(1)}, f32[2,8,1024,64,8]{2,3,4,1,0:T(8,128)}) fusion(pred[2,8,64,1024]{3,2,1,0:T(8,128)(4,1)S(1)} %broadcast_compare_fusion.4, bf16[2,8,1024,128,1]{3,2,4,1,0:T(8,128)(2,1)} %bitcast.133, bf16[1,2,64,8,8,128]{5,4,3,2,1,0:T(8,128)(2,1)S(1)} %constant_dynamic-slice_fusion.3), kind=kOutput, calls=%fused_computation.9.clone.1 | convolution fusion | flops 2172641280 | bytes 40927232 | tf_op jit(solution)/shard_map/while/body/eval_jaxpr/tqhgd,tgkd->tghqk/dot_general | solution.py:95
  426.8 14.9 %fusion.69 = f32[2,8,8,64]{3,2,1,0:T(8,128)S(1)} fusion(f32[2,8,1024,64,8]{2,3,4,1,0:T(8,128)} %get-tuple-element.187, f32[2,8,8,64]{3,2,1,0:T(8,128)S(1)} %get-tuple-element.188, pred[2,8,64,1024]{3,2,1,0:T(8,128)(4,1)S(1)} %broadcast_compare_fusion.4), kind=kLoop, calls=%fused_computation.7.clone.1 | loop fusion | flops 33546240 | bytes 34668544 | tf_op jit(solution)/shard_map/while/body/eval_jaxpr/reduce_sum | solution.py:15
  441.7 6.0 %gather_fusion.1 = bf16[256,64,128]{2,1,0:T(8,128)(2,1)} fusion(bf16[8,40,64,128]{3,2,1,0:T(8,128)(2,1)} %get-tuple-element.210, s32[256]{0:T(256)S(1)} %reshape.347), kind=kCustom, calls=%fused_computation.clone.clone.1 | custom fusion | bytes 8390656 | tf_op jit(solution)/shard_map/while/body/eval_jaxpr/gather | solution.py:88
  447.6 15.8 %fusion.70 = bf16[1,2,64,8,8,128]{5,2,3,4,1,0:T(8,128)(2,1)S(1)} fusion(f32[2,64,8,8]{1,2,3,0:T(8,128)S(1)} %bitcast.145, bf16[2,8,1024,128,1]{3,2,4,1,0:T(8,128)(2,1)} %bitcast.134, f32[2,8,1024,64,8]{2,3,4,1,0:T(8,128)} %get-tuple-element.187, f32[2,8,8,64]{3,2,1,0:T(8,128)S(1)} %get-tuple-element.188, ...), kind=kOutput, calls=%fused_computation.18.clone.1 | convolution fusion | flops 2183135232 | bytes 40960000 | tf_op jit(solution)/shard_map/while/body/eval_jaxpr/tghqk,tgkd->tqhgd/dot_general | solution.py:102
  463.4 2.7 copy_dynamic-update-slice_fusion.2
  466.2 0.1 add.210
  466.4 0.6 broadcast_compare_fusion.4
  467.2 6.0 %gather_fusion = bf16[256,64,128]{2,1,0:T(8,128)(2,1)} fusion(bf16[8,40,64,128]{3,2,1,0:T(8,128)(2,1)} %get-tuple-element.213, s32[256]{0:T(256)S(1)} %reshape.347), kind=kCustom, calls=%fused_computation.1.clone.clone.1 | custom fusion | bytes 8390656 | tf_op jit(solution)/shard_map/while/body/eval_jaxpr/gather | solution.py:85
  473.2 1.8 constant_dynamic-slice_fusion.3
  474.9 16.8 %fusion.68 = (f32[2,8,8,64]{3,2,1,0:T(8,128)S(1)}, f32[2,8,1024,64,8]{2,3,4,1,0:T(8,128)}) fusion(pred[2,8,64,1024]{3,2,1,0:T(8,128)(4,1)S(1)} %broadcast_compare_fusion.4, bf16[2,8,1024,128,1]{3,2,4,1,0:T(8,128)(2,1)} %bitcast.133, bf16[1,2,64,8,8,128]{5,4,3,2,1,0:T(8,128)(2,1)S(1)} %constant_dynamic-slice_fusion.3), kind=kOutput, calls=%fused_computation.9.clone.1 | convolution fusion | flops 2172641280 | bytes 40927232 | tf_op jit(solution)/shard_map/while/body/eval_jaxpr/tqhgd,tgkd->tghqk/dot_general | solution.py:95
  491.7 14.9 %fusion.69 = f32[2,8,8,64]{3,2,1,0:T(8,128)S(1)} fusion(f32[2,8,1024,64,8]{2,3,4,1,0:T(8,128)} %get-tuple-element.187, f32[2,8,8,64]{3,2,1,0:T(8,128)S(1)} %get-tuple-element.188, pred[2,8,64,1024]{3,2,1,0:T(8,128)(4,1)S(1)} %broadcast_compare_fusion.4), kind=kLoop, calls=%fused_computation.7.clone.1 | loop fusion | flops 33546240 | bytes 34668544 | tf_op jit(solution)/shard_map/while/body/eval_jaxpr/reduce_sum | solution.py:15
  506.6 6.0 %gather_fusion.1 = bf16[256,64,128]{2,1,0:T(8,128)(2,1)} fusion(bf16[8,40,64,128]{3,2,1,0:T(8,128)(2,1)} %get-tuple-element.210, s32[256]{0:T(256)S(1)} %reshape.347), kind=kCustom, calls=%fused_computation.clone.clone.1 | custom fusion | bytes 8390656 | tf_op jit(solution)/shard_map/while/body/eval_jaxpr/gather | solution.py:88
  512.6 15.8 %fusion.70 = bf16[1,2,64,8,8,128]{5,2,3,4,1,0:T(8,128)(2,1)S(1)} fusion(f32[2,64,8,8]{1,2,3,0:T(8,128)S(1)} %bitcast.145, bf16[2,8,1024,128,1]{3,2,4,1,0:T(8,128)(2,1)} %bitcast.134, f32[2,8,1024,64,8]{2,3,4,1,0:T(8,128)} %get-tuple-element.187, f32[2,8,8,64]{3,2,1,0:T(8,128)S(1)} %get-tuple-element.188, ...), kind=kOutput, calls=%fused_computation.18.clone.1 | convolution fusion | flops 2183135232 | bytes 40960000 | tf_op jit(solution)/shard_map/while/body/eval_jaxpr/tghqk,tgkd->tqhgd/dot_general | solution.py:102
  528.4 2.7 copy_dynamic-update-slice_fusion.2
  531.1 0.1 add.210
  531.3 0.6 broadcast_compare_fusion.4
  532.2 6.0 %gather_fusion = bf16[256,64,128]{2,1,0:T(8,128)(2,1)} fusion(bf16[8,40,64,128]{3,2,1,0:T(8,128)(2,1)} %get-tuple-element.213, s32[256]{0:T(256)S(1)} %reshape.347), kind=kCustom, calls=%fused_computation.1.clone.clone.1 | custom fusion | bytes 8390656 | tf_op jit(solution)/shard_map/while/body/eval_jaxpr/gather | solution.py:85
  538.1 1.8 constant_dynamic-slice_fusion.3
  539.9 16.8 %fusion.68 = (f32[2,8,8,64]{3,2,1,0:T(8,128)S(1)}, f32[2,8,1024,64,8]{2,3,4,1,0:T(8,128)}) fusion(pred[2,8,64,1024]{3,2,1,0:T(8,128)(4,1)S(1)} %broadcast_compare_fusion.4, bf16[2,8,1024,128,1]{3,2,4,1,0:T(8,128)(2,1)} %bitcast.133, bf16[1,2,64,8,8,128]{5,4,3,2,1,0:T(8,128)(2,1)S(1)} %constant_dynamic-slice_fusion.3), kind=kOutput, calls=%fused_computation.9.clone.1 | convolution fusion | flops 2172641280 | bytes 40927232 | tf_op jit(solution)/shard_map/while/body/eval_jaxpr/tqhgd,tgkd->tghqk/dot_general | solution.py:95
  556.7 14.9 %fusion.69 = f32[2,8,8,64]{3,2,1,0:T(8,128)S(1)} fusion(f32[2,8,1024,64,8]{2,3,4,1,0:T(8,128)} %get-tuple-element.187, f32[2,8,8,64]{3,2,1,0:T(8,128)S(1)} %get-tuple-element.188, pred[2,8,64,1024]{3,2,1,0:T(8,128)(4,1)S(1)} %broadcast_compare_fusion.4), kind=kLoop, calls=%fused_computation.7.clone.1 | loop fusion | flops 33546240 | bytes 34668544 | tf_op jit(solution)/shard_map/while/body/eval_jaxpr/reduce_sum | solution.py:15
  571.6 6.0 %gather_fusion.1 = bf16[256,64,128]{2,1,0:T(8,128)(2,1)} fusion(bf16[8,40,64,128]{3,2,1,0:T(8,128)(2,1)} %get-tuple-element.210, s32[256]{0:T(256)S(1)} %reshape.347), kind=kCustom, calls=%fused_computation.clone.clone.1 | custom fusion | bytes 8390656 | tf_op jit(solution)/shard_map/while/body/eval_jaxpr/gather | solution.py:88
  577.5 15.8 %fusion.70 = bf16[1,2,64,8,8,128]{5,2,3,4,1,0:T(8,128)(2,1)S(1)} fusion(f32[2,64,8,8]{1,2,3,0:T(8,128)S(1)} %bitcast.145, bf16[2,8,1024,128,1]{3,2,4,1,0:T(8,128)(2,1)} %bitcast.134, f32[2,8,1024,64,8]{2,3,4,1,0:T(8,128)} %get-tuple-element.187, f32[2,8,8,64]{3,2,1,0:T(8,128)S(1)} %get-tuple-element.188, ...), kind=kOutput, calls=%fused_computation.18.clone.1 | convolution fusion | flops 2183135232 | bytes 40960000 | tf_op jit(solution)/shard_map/while/body/eval_jaxpr/tghqk,tgkd->tqhgd/dot_general | solution.py:102
  593.3 2.7 copy_dynamic-update-slice_fusion.2
  (59 shorter events, 1.9 us)
Async XLA Ops:
  4.0 10.7 %all-to-all-start = ((s32[8,16,2]{0,2,1:T(2,128)}), s32[8,16,2]{0,2,1:T(2,128)S(1)}, u32[]{:S(2)}, u32[]{:S(2)}) async-start(s32[8,16,2]{0,2,1:T(2,128)} %copy.57), calls=%async_computation | async-start | bytes 32768 | tf_op jit(solution)/shard_map/all_to_all | solution.py:69
  38.9 7.2 %copy-start.1 = (bf16[1,8,8,128]{3,2,1,0:T(8,128)(2,1)S(1)}, bf16[1,8,8,128]{3,2,1,0:T(8,128)(2,1)}, u32[]{:S(2)}) copy-start(bf16[1,8,8,128]{3,2,1,0:T(8,128)(2,1)} %param.10) | copy-start | bytes 49156
  38.9 283.5 %all-to-all-start.1 = ((bf16[8,16,2,64,256]{4,3,2,0,1:T(8,128)(2,1)}), bf16[8,16,2,64,256]{4,3,2,0,1:T(8,128)(2,1)}, u32[]{:S(2)}, u32[]{:S(2)}) async-start(bf16[8,16,2,64,256]{4,3,2,0,1:T(8,128)(2,1)} %copy.62), calls=%async_computation.1 | async-start | bytes 16777216 | tf_op jit(solution)/shard_map/all_to_all | solution.py:74
  295.3 23.4 %copy-start = (s32[1,8,8,16]{3,2,1,0:T(8,128)S(1)}, s32[1,8,8,16]{3,2,1,0:T(8,128)}, u32[]{:S(2)}) copy-start(s32[1,8,8,16]{3,2,1,0:T(8,128)} %param.11) | copy-start | bytes 12292
where the time goes:
time: 604 us; the launch traced here: 596 us
  blocking collectives  192 us (32%)
  matrix products  170 us (28%)
  other arithmetic  121 us (20%)
  local copies, waits for them, and re-layouts  97 us (16%)
  starting transfers between devices  13.6 us (2%)
    all_gather x1, blocking collectives, local(): lax.all_gather(compressed, 'seq', axis=1, tiled=True)[0]  192 us
    dot_general x4, matrix products, attend(): jnp.einsum('tqhgd,tgkd->tghqk', query_part, key_sel, preferred_element_ty...  67.3 us
    dot_general x4, matrix products, attend(): jnp.einsum('tghqk,tgkd->tqhgd', rounded, value_sel, preferred_element_typ...  63 us
    reduce_sum x4, other arithmetic, softmax_parts(): return (weights, jnp.sum(weights, axis=-1, keepdims=True))  59.5 us
    dot_general x1, matrix products, local(): jnp.einsum('tjgd,ngd->tjgn', query_rows, lax.all_gather(compressed, 'seq'...  39.5 us
    gather x4, local copies, waits for them, and re-layouts, attend(): value_pool[group_sel, index_part]  23.9 us
    gather x4, local copies, waits for them, and re-layouts, attend(): key_pool[group_sel, index_part]  23.9 us
    sub x1, other arithmetic, softmax_parts(): weights = jnp.exp(scores - row_top)  20.3 us
  transfers between devices with their start and end apart: 2, of which 1 were waited for; matrix products, arithmetic and copies ran while one was open for 15% of the time, Pallas kernels for 0%

commit v1 on v0

v1 whole, which is shorter than its diff:
```python
import functools
import math

import jax
import jax.numpy as jnp
from jax import lax
from jax.experimental import pallas as pl
from jax.experimental.pallas import tpu as pltpu
from jax.sharding import PartitionSpec as P

HPG = 8
BLOCK = 64
TOPN = 16
CAP = 2


def softmax_parts(scores):
    row_top = jnp.max(scores, axis=-1, keepdims=True)
    weights = jnp.exp(scores - row_top)
    return (weights, jnp.sum(weights, axis=-1, keepdims=True))


def attend_tile(shape, slot_ref, pick_ref, first_ref, query_ref, own_ref, remote_ref, out_ref, pool, picked):
    heads_local, blk_dev, shards, cap, block_len, head_width = shape
    group, tile = pl.program_id(0), pl.program_id(1)

    @pl.when(tile == 0)
    def _():
        pool[:blk_dev] = own_ref[0]
        for shard in range(shards):
            pool[blk_dev + shard * cap : blk_dev + (shard + 1) * cap] = remote_ref[shard, 0]

    tile_number = first_ref[0] + tile
    keys = TOPN * block_len
    column = lax.broadcasted_iota(jnp.int32, (1, keys), 1)
    within = column % block_len
    block_place = column // block_len
    limit = jnp.full((1, keys), -1, jnp.int32)
    for place in range(TOPN):
        picked[place * block_len : (place + 1) * block_len] = pool[slot_ref[tile, group, place]]
        is_own = pick_ref[tile, group, place] == tile_number
        limit = jnp.where((block_place == place) & is_own, within, limit)
    rows = block_len * heads_local
    part = min(rows, 256)
    factor = math.log2(math.e) * head_width ** (-0.5)
    for start in range(0, rows, part):
        query = query_ref[0, 0, start : start + part]
        scores = lax.dot_general(
            query,
            picked[:, :head_width],
            (((1,), (1,)), ((), ())),
            preferred_element_type=jnp.float32,
        )
        token = (start + lax.broadcasted_iota(jnp.int32, (part, 1), 0)) // heads_local
        scores = jnp.where(limit <= token, scores, -jnp.inf)
        row_top = jnp.max(scores, axis=-1, keepdims=True)
        weights = jnp.exp2((scores - row_top) * factor)
        totals = jnp.sum(weights, axis=-1, keepdims=True)
        mixed = jnp.dot(
            weights.astype(jnp.bfloat16),
            picked[:, head_width:],
            preferred_element_type=jnp.float32,
        )
        out_ref[0, 0, start : start + part] = (mixed / totals).astype(jnp.bfloat16)


def local(queries, key_rows, value_rows, compressed, chosen):
    _, tok_rows, heads_local, groups, head_width = queries.shape
    block_len = BLOCK
    shards = lax.axis_size("seq")
    seq_rank = lax.axis_index("seq")
    blk_dev = tok_rows // block_len
    nblk = blk_dev * shards
    score_scale = head_width ** (-0.5)
    query_rows = queries[0]
    query_pos = seq_rank * tok_rows + jnp.arange(tok_rows, dtype=jnp.int32)
    gathered = lax.all_gather(compressed, "seq", axis=1, tiled=True)
    logits = (
        jnp.einsum(
            "tjgd,ngd->tjgn",
            query_rows,
            gathered[0],
            preferred_element_type=jnp.float32,
        )
        * score_scale
    )
    all_blocks = jnp.arange(nblk, dtype=jnp.int32)
    seen = all_blocks[None, :] <= (query_pos // block_len)[:, None]
    logits = jnp.where(seen[:, None, None, :], logits, -jnp.inf)
    weights, totals = softmax_parts(logits)
    probability = weights / totals
    pooled = jnp.sum(
        probability.reshape(blk_dev, block_len, heads_local, groups, nblk), axis=(1, 2)
    )[None]
    shared = lax.psum_scatter(
        pooled.astype(jnp.bfloat16), "head", scatter_dimension=2, tiled=True
    ).astype(jnp.float32)
    tile_ids = seq_rank * blk_dev + jnp.arange(blk_dev, dtype=jnp.int32)
    factor = (tile_ids + 1).astype(jnp.float32) / (block_len * HPG)
    block_scores = shared * factor[None, :, None, None]
    pick_rows = chosen[0]
    onehot = pick_rows[..., None] == all_blocks
    needed = jnp.any(onehot, axis=(0, 2))
    owner_of = all_blocks // blk_dev
    needed = needed & (owner_of != seq_rank)[None, :]
    needed_grid = needed.reshape(groups, shards, blk_dev).astype(jnp.int32)
    rank_in = jnp.cumsum(needed_grid, axis=2) - needed_grid
    places = jnp.arange(CAP, dtype=jnp.int32)
    within = jnp.arange(blk_dev, dtype=jnp.int32)
    matched = (needed_grid[..., None] == 1) & (rank_in[..., None] == places)
    wanted = jnp.sum(jnp.where(matched, within[:, None], 0), axis=2)
    slot_of = blk_dev + owner_of[None, :] * CAP + rank_in.reshape(groups, nblk)
    slot_of = jnp.where(
        owner_of[None, :] == seq_rank, all_blocks[None, :] - seq_rank * blk_dev, slot_of
    )
    pool_index = jnp.sum(jnp.where(onehot, slot_of[None, :, None, :], 0), axis=3)
    key_local = key_rows[0].reshape(blk_dev, block_len, groups, head_width)
    value_local = value_rows[0].reshape(blk_dev, block_len, groups, head_width)
    own_rows = jnp.transpose(jnp.concatenate([key_local, value_local], axis=-1), (2, 0, 1, 3))
    requested = lax.all_to_all(
        jnp.transpose(wanted, (1, 0, 2)), "seq", split_axis=0, concat_axis=0, tiled=True
    )
    group_ids = jnp.arange(groups, dtype=jnp.int32)[None, :, None]
    found = jnp.take(
        own_rows.reshape(groups * blk_dev, block_len, 2 * head_width),
        group_ids * blk_dev + requested,
        axis=0,
        mode="clip",
    )
    found, _ = lax.optimization_barrier((found, gathered))
    fetched = lax.all_to_all(found, "seq", split_axis=0, concat_axis=0, tiled=True)
    rows = block_len * heads_local
    query_tiles = jnp.transpose(
        query_rows.reshape(blk_dev, rows, groups, head_width), (2, 0, 1, 3)
    )
    shape = (heads_local, blk_dev, shards, CAP, block_len, head_width)
    tile_spec = pl.BlockSpec((1, 1, rows, head_width), lambda g, t, *_: (g, t, 0, 0))
    attended = pl.pallas_call(
        functools.partial(attend_tile, shape),
        grid_spec=pltpu.PrefetchScalarGridSpec(
            num_scalar_prefetch=3,
            grid=(groups, blk_dev),
            in_specs=[
                tile_spec,
                pl.BlockSpec(
                    (1, blk_dev, block_len, 2 * head_width), lambda g, t, *_: (g, 0, 0, 0)
                ),
                pl.BlockSpec(
                    (shards, 1, CAP, block_len, 2 * head_width),
                    lambda g, t, *_: (0, g, 0, 0, 0),
                ),
            ],
            out_specs=tile_spec,
            scratch_shapes=[
                pltpu.VMEM((blk_dev + shards * CAP, block_len, 2 * head_width), jnp.bfloat16),
                pltpu.VMEM((TOPN * block_len, 2 * head_width), jnp.bfloat16),
            ],
        ),
        out_shape=jax.ShapeDtypeStruct((groups, blk_dev, rows, head_width), jnp.bfloat16),
        compiler_params=pltpu.CompilerParams(
            dimension_semantics=("arbitrary", "arbitrary"), vmem_limit_bytes=48 * 1024 * 1024
        ),
    )(pool_index, pick_rows, (seq_rank * blk_dev)[None], query_tiles, own_rows, fetched)
    attended = jnp.transpose(attended, (1, 2, 0, 3))
    attended = attended.reshape(1, tok_rows, heads_local, groups, head_width)
    return (block_scores, attended)


def solution(mesh):
    placed = (
        P("batch", "seq", "head", None, None),
        P("batch", "seq", None, None),
        P("batch", "seq", None, None),
        P("batch", "seq", None, None),
        P("batch", "seq", None, None),
    )
    return jax.shard_map(
        local,
        mesh=mesh,
        in_specs=placed,
        out_specs=(P("batch", "seq", "head", None), P("batch", "seq", "head", None, None)),
        check_vma=False,
    )
```

time: 604 us -> 341 us (0.56)
  blocking collectives: 192 us -> 15.9 us
  matrix products: 170 us -> 38.4 us
  waiting for transfers between devices: 1.42 us -> 91.4 us
  Pallas kernels: 0 us -> 83.3 us
  other arithmetic: 121 us -> 45.6 us
  local copies, waits for them, and re-layouts: 97 us -> 42.2 us
    all_gather x1, blocking collectives: 192 us -> 15.9 us  [local(): gathered = lax.all_gather(compressed, 'seq', axis=1, tiled=True)]
    dot_general x9 -> x1, matrix products: 170 us -> 38.4 us  [local(): jnp.einsum('tjgd,ngd->tjgn', query_rows, gathered[0], preferred_element_t...]
    all_to_all x2, waiting for transfers between devices: 1.42 us -> 91.4 us  [the longest x1 91.4 us: local(): lax.all_to_all(found, 'seq', split_axis=0, concat_axis=0, tiled=True)]
    pallas_call x0 -> x1, Pallas kernels: none -> 83.3 us  [local(): pl.pallas_call(functools.partial(attend_tile, shape), grid_spec=pltpu.Pre...]
    reduce_sum x4 -> x0, other arithmetic: 59.5 us -> none  [softmax_parts(): return (weights, jnp.sum(weights, axis=-1, keepdims=True))]
    gather x10 -> x1, local copies, waits for them, and re-layouts: 54.4 us -> 10.1 us  [local(): jnp.take(own_rows.reshape(groups * blk_dev, block_len, 2 * head_width), g...]
    unnamed x9 -> x7, local copies, waits for them, and re-layouts: 6.4 us -> 27.8 us
    concatenate x11 -> x1, other arithmetic: 14.8 us -> 1.79 us  [local(): jnp.concatenate([key_local, value_local], axis=-1)]
  transfers between devices with their start and end apart: 2 -> 2, of which waited for: 1 -> 1; matrix products, arithmetic and copies ran while one was open for 15% -> 29% of each run, Pallas kernels for 0% -> 0%
where the time goes in v1:
time: 341 us; the launch traced here: 336 us
  waiting for transfers between devices  91.4 us (27%)
  Pallas kernels  83.3 us (24%)
  other arithmetic  45.6 us (13%)
  local copies, waits for them, and re-layouts  42.2 us (12%)
  matrix products  38.4 us (11%)
  starting transfers between devices  18 us (5%)
  blocking collectives  15.9 us (5%)
    all_to_all x1, waiting for transfers between devices, local(): lax.all_to_all(found, 'seq', split_axis=0, concat_axis=0, tiled=True)  91.4 us
    pallas_call x1, Pallas kernels, local(): pl.pallas_call(functools.partial(attend_tile, shape), grid_spec=pltpu.Pre...  83.3 us
    dot_general x1, matrix products, local(): jnp.einsum('tjgd,ngd->tjgn', query_rows, gathered[0], preferred_element_t...  38.4 us
    unnamed x7, local copies, waits for them, and re-layouts  27.8 us
    sub x1, other arithmetic, softmax_parts(): weights = jnp.exp(scores - row_top)  20.3 us
    div x1, other arithmetic, local(): probability = weights / totals  17.2 us
    all_gather x1, blocking collectives, local(): gathered = lax.all_gather(compressed, 'seq', axis=1, tiled=True)  15.9 us
    all_to_all x1, starting transfers between devices, local(): lax.all_to_all(found, 'seq', split_axis=0, concat_axis=0, tiled=True)  11.5 us
  transfers between devices with their start and end apart: 2, of which 1 were waited for; matrix products, arithmetic and copies ran while one was open for 29% of the time, Pallas kernels for 0%

profile of v1, /device:TPU:15, one launch (start us, length us, event | category | flops | bytes accessed | tf_op | source)
XLA Modules:
  0.0 335.7 jit_solution(2306429952923470894)
XLA Ops:
  0.6 1.0 fusion.8
  1.6 0.1 reduce_or.12
  1.8 1.3 reduce_window_sum.13
  3.1 0.1 copy.52
  3.2 0.1 copy.51
  3.3 0.7 copy.53
  4.0 6.5 %all-to-all-start = ((s32[16,8,2]{1,2,0:T(2,128)}), s32[16,8,2]{1,2,0:T(2,128)S(1)}, u32[]{:S(2)}, u32[]{:S(2)}) async-start(s32[16,8,2]{1,2,0:T(2,128)} %copy.53), calls=%async_computation | async-start | bytes 32768 | tf_op jit(solution)/shard_map/all_to_all | solution.py:120
  10.5 0.7 copy.45
  11.2 15.9 %all_gather.3 = bf16[1,128,8,128]{3,1,2,0:T(8,128)(2,1)S(1)} all-gather(bf16[1,8,8,128]{3,1,2,0:T(8,128)(2,1)S(1)} %copy.45), channel_id=1, replica_groups=mesh['seq'=16,'head'=1,'batch'=2] {'seq'}, dimensions={1}, use_global_device_ids=true | all-gather | bytes 278528 | tf_op jit(solution)/shard_map/all_gather | solution.py:77
  27.1 1.4 copy.50
  28.5 1.4 copy.49
  29.9 1.8 pad_maximum_fusion
  31.7 0.0 all-to-all-done
  31.7 0.1 copy.54
  31.7 0.1 broadcast_add_fusion
  31.8 0.1 copy.55
  31.9 0.1 reshape.215
  32.1 10.1 %gather_fusion = bf16[256,64,256]{2,1,0:T(8,128)(2,1)} fusion(bf16[64,64,256]{2,1,0:T(8,128)(2,1)} %bitcast.46, s32[1024]{0:T(1024)S(1)} %pad_clamp_fusion), kind=kCustom, calls=%fused_computation | custom fusion | bytes 16778240 | tf_op jit(solution)/shard_map/jit(_take)/gather | solution.py:124
  42.2 11.5 %all-to-all-start.1 = ((bf16[16,8,2,64,256]{4,3,2,1,0:T(8,128)(2,1)}), bf16[16,8,2,64,256]{4,3,2,1,0:T(8,128)(2,1)}, u32[]{:S(2)}, u32[]{:S(2)}) async-start(bf16[16,8,2,64,256]{4,3,2,1,0:T(8,128)(2,1)} %bitcast.48), calls=%async_computation.1 | async-start | bytes 16777216 | tf_op jit(solution)/shard_map/all_to_all | solution.py:131
  53.7 0.1 reduce_window_sum.14
  53.8 7.9 %copy.48 = bf16[1,512,8,8,128]{4,2,1,3,0:T(8,128)(2,1)} copy(bf16[1,512,8,8,128]{4,3,2,1,0:T(8,128)(2,1)} %param.5) | data formatting | bytes 16777216 | tf_op args[0]
  61.7 38.4 %fusion.3 = f32[8,128,512,8]{2,1,3,0:T(8,128)} fusion(bf16[512,8,8,128]{3,2,1,0:T(8,128)(2,1)} %bitcast.47, bf16[1,128,8,128]{3,1,2,0:T(8,128)(2,1)S(1)} %all_gather.3), kind=kOutput, calls=%fused_computation.7 | convolution fusion | flops 1073741824 | bytes 25427968 | tf_op jit(solution)/shard_map/tjgd,ngd->tjgn/dot_general | solution.py:79
  100.1 17.2 %fusion = f32[512,8,8,128]{0,3,1,2:T(8,128)} fusion(f32[8,128,512,8]{2,1,3,0:T(8,128)} %fusion.3, pred[512,128]{0,1:T(8,128)(4,1)S(1)} %iota_compare_fusion.1), kind=kOutput, calls=%fused_computation.1 | output fusion | flops 21037312 | bytes 33619968 | tf_op jit(solution)/shard_map/div | solution.py:91
  117.3 0.0 copy-start
  117.3 20.3 %divide_reduce_fusion = f32[512,8,128]{0,2,1:T(8,128)} fusion(f32[512,8,8,128]{0,3,1,2:T(8,128)} %fusion, f32[8,128,512,8]{2,1,3,0:T(8,128)} %fusion.3, pred[512,128]{0,1:T(8,128)(4,1)S(1)} %iota_compare_fusion.1), kind=kOutput, calls=%fused_computation.5 | output fusion | flops 28868736 | bytes 35717120 | tf_op jit(solution)/shard_map/sub | solution.py:19
  137.6 3.0 copy.47
  140.6 0.0 copy-done
  140.6 1.3 select_reduce_fusion.slot_ref
  142.0 1.7 bitcast_reduce_fusion
  143.6 0.7 convert_multiply_fusion
  144.3 91.4 %all-to-all-done.1.remote_ref = bf16[16,8,2,64,256]{4,3,2,1,0:T(8,128)(2,1)} async-done(((bf16[16,8,2,64,256]{4,3,2,1,0:T(8,128)(2,1)}), bf16[16,8,2,64,256]{4,3,2,1,0:T(8,128)(2,1)}, u32[]{:S(2)}, u32[]{:S(2)}) %all-to-all-start.1) | async-done | bytes 8388640 | tf_op jit(solution)/shard_map/all_to_all | solution.py:131
  235.7 83.3 %shard_map.68 = bf16[8,8,512,128]{3,2,1,0:T(8,128)(2,1)} custom-call(s32[8,8,16]{2,1,0:T(8,128)S(1)} %select_reduce_fusion.slot_ref, s32[8,8,16]{2,1,0:T(8,128)S(1)} %bitcast.45, s32[1]{0:T(128)} %bitcast.8.first_ref, bf16[8,8,512,128]{3,2,1,0:T(8,128)(2,1)} %bitcast.49, bf16[8,8,64,256]{3,2,1,0:T(8,128)(2,1)S(1)} %get-tuple-element.17.own_ref, ...), custom_call_target="tpu_custom_call" | custom-call | tf_op jit(solution)/shard_map/pallas_call | solution.py:138
  319.0 16.5 %copy.56 = bf16[1,512,8,8,128]{4,3,2,1,0:T(8,128)(2,1)} copy(bf16[1,512,8,8,128]{4,2,1,3,0:T(8,128)(2,1)} %bitcast.50) | data formatting | bytes 16777216
  (12 shorter events, 0.2 us)
Async XLA Ops:
  4.0 27.7 %all-to-all-start = ((s32[16,8,2]{1,2,0:T(2,128)}), s32[16,8,2]{1,2,0:T(2,128)S(1)}, u32[]{:S(2)}, u32[]{:S(2)}) async-start(s32[16,8,2]{1,2,0:T(2,128)} %copy.53), calls=%async_computation | async-start | bytes 32768 | tf_op jit(solution)/shard_map/all_to_all | solution.py:120
  42.2 193.5 %all-to-all-start.1 = ((bf16[16,8,2,64,256]{4,3,2,1,0:T(8,128)(2,1)}), bf16[16,8,2,64,256]{4,3,2,1,0:T(8,128)(2,1)}, u32[]{:S(2)}, u32[]{:S(2)}) async-start(bf16[16,8,2,64,256]{4,3,2,1,0:T(8,128)(2,1)} %bitcast.48), calls=%async_computation.1 | async-start | bytes 16777216 | tf_op jit(solution)/shard_map/all_to_all | solution.py:131
  117.3 23.3 %copy-start = (s32[1,8,8,16]{3,2,1,0:T(8,128)S(1)}, s32[1,8,8,16]{3,2,1,0:T(8,128)}, u32[]{:S(2)}) copy-start(s32[1,8,8,16]{3,2,1,0:T(8,128)} %param.9) | copy-start | bytes 12292
